TPU v7x, 8 devices: a whole 2x2x1 slice. The times are simulated.
8 devices in a mesh: dp: 2 (over z, y), dcp: 4 (over x, core).
Axes of the slice: x: 2, y: 2, z: 1, core: 2. Of those that a mesh axis runs over, the one named last changes fastest.
Arguments:
- q_abs: bfloat16 [128, 2, 64, 576], P('dp', None, 'dcp'), parts along dimension 0
- kv_cache: bfloat16 [128, 32, 4, 64, 576], P('dp', None, 'dcp'), parts along dimension 0
- lengths: int32 [128], P('dp'), parts along dimension 0
Outputs:
- output: bfloat16 [128, 2, 64, 512], P('dp', None, 'dcp'), parts along dimension 0
There are 2 independent parts. A program takes and returns all parts, laid end to end along the dimension named above; each array names one.
All inputs are finite; a program needn't handle non-finite values.
Results may differ from a plain program's by a relative error of at most 0.00787497.
Values are sent between devices in bfloat16 or wider.
A program may use at most 1 GiB of HBM per device.

v0:
```python
import jax
import jax.numpy as jnp
from jax import lax
from jax.sharding import PartitionSpec as P

LATENT = 512
ROPE = 64
NOPE = 128
PAGE = 64
MASKED = -1e30


def solution(mesh):
    group_size = mesh.shape['dcp']
    score_scale = (NOPE + ROPE) ** -0.5

    def local_step(q_blk, kv_blk, len_blk):
        batch_loc, tok_count, heads_loc, q_width = q_blk.shape
        rounds = kv_blk.shape[1]
        local_keys = kv_blk.reshape(batch_loc, rounds * PAGE, q_width)
        q_all = lax.all_gather(q_blk, 'dcp', axis=2, tiled=True)
        scores = jnp.einsum('bthd,bsd->bths', q_all, local_keys, preferred_element_type=jnp.float32) * score_scale
        device = lax.axis_index('dcp')
        positions = ((jnp.arange(rounds)[:, None] * group_size + device) * PAGE + jnp.arange(PAGE)[None, :]).reshape(rounds * PAGE)
        last_pos = len_blk[:, None] - tok_count + jnp.arange(tok_count)[None, :]
        visible = positions[None, None, None, :] <= last_pos[:, :, None, None]
        scores = jnp.where(visible, scores, MASKED)
        row_max = jnp.max(scores, axis=-1)
        weights = jnp.exp(scores - row_max[..., None])
        row_sum = jnp.sum(weights, axis=-1)
        part_out = jnp.einsum('bths,bsc->bthc', weights.astype(jnp.bfloat16), local_keys[:, :, :LATENT], preferred_element_type=jnp.float32)
        part_out = (part_out / row_sum[..., None]).astype(jnp.bfloat16)
        part_lse = row_max + jnp.log(row_sum)
        recv_out = lax.all_to_all(part_out, 'dcp', 2, 2, tiled=True).reshape(batch_loc, tok_count, group_size, heads_loc, LATENT)
        recv_lse = lax.all_to_all(part_lse, 'dcp', 2, 2, tiled=True).reshape(batch_loc, tok_count, group_size, heads_loc)
        total_lse = jax.nn.logsumexp(recv_lse, axis=2, keepdims=True)
        merge_w = jnp.exp(recv_lse - total_lse)
        merged = jnp.sum(merge_w[..., None] * recv_out.astype(jnp.float32), axis=2)
        return merged.astype(jnp.bfloat16)

    return jax.shard_map(local_step, mesh=mesh, in_specs=(P('dp', None, 'dcp', None), P('dp', None, 'dcp', None, None), P('dp')), out_specs=P('dp', None, 'dcp', None), check_vma=False)
```

profile of v0, /device:TPU:0, one launch (start us, length us, event | category | flops | bytes accessed | tf_op | source)
XLA Modules:
  0.0 399.8 jit_solution(5131314937804041325)
XLA Ops:
  6.5 0.0 all-gather.2.cloned.1.call-start
  6.5 0.7 all-gather.2.cloned.1.call-update
  7.3 0.1 iota_add_fusion.1
  7.3 0.1 add.66
  7.4 0.7 broadcast_add_fusion
  8.1 0.1 iota_add_fusion
  8.2 0.7 broadcast_compare_fusion
  8.8 70.7 %all-gather.2.cloned.1.call-done = bf16[64,2,64,576]{3,2,1,0:T(8,128)(2,1)} async-done(((bf16[64,2,16,576]{3,2,1,0:T(8,128)(2,1)}), bf16[64,2,64,576]{3,2,1,0:T(8,128)(2,1)}) %all-gather.2.cloned.1.call-update) | async-done | bytes 9437200 | tf_op jit(solution)/shard_map/all_gather | solution.py:21
  79.6 90.5 %fusion.1 = (f32[64,2,64]{2,1,0:T(2,128)S(1)}, f32[64,2,64,2048]{3,2,1,0:T(8,128)}) fusion(pred[64,2,2048]{2,1,0:T(4,128)(4,1)S(1)} %broadcast_compare_fusion, bf16[64,2,64,576]{3,2,1,0:T(8,128)(2,1)} %all-gather.2.cloned.1.call-done, bf16[64,2048,576,1]{2,1,3,0:T(8,128)(2,1)} %bitcast.7), kind=kOutput, calls=%fused_computation.4 | convolution fusion | flops 19377676288 | bytes 227835904 | tf_op jit(solution)/shard_map/bthd,bsd->bths/dot_general | solution.py:22
  170.1 21.5 %fusion.3 = f32[64,2,64]{2,1,0:T(2,128)S(1)} fusion(f32[64,2,64,2048]{3,2,1,0:T(8,128)} %get-tuple-element.6, f32[64,2,64]{2,1,0:T(2,128)S(1)} %get-tuple-element.5, pred[64,2,2048]{2,1,0:T(4,128)(4,1)S(1)} %broadcast_compare_fusion), kind=kLoop, calls=%fused_computation.6 | loop fusion | flops 67100672 | bytes 67436544 | tf_op jit(solution)/shard_map/reduce_sum | solution.py:30
  191.6 0.1 copy.23
  191.7 0.7 reshape.89
  192.4 3.3 all-to-all-start
  195.7 65.4 %divide_convert_fusion = bf16[64,2,64,512]{3,2,1,0:T(8,128)(2,1)} fusion(bf16[64,2048,576]{2,1,0:T(8,128)(2,1)} %bitcast, f32[64,2,64,2048]{3,2,1,0:T(8,128)} %get-tuple-element.6, f32[64,2,64]{2,1,0:T(2,128)S(1)} %get-tuple-element.5, pred[64,2,2048]{2,1,0:T(4,128)(4,1)S(1)} %broadcast_compare_fusion, f32[64,2,64]{2,1,0:T(2,128)S(1)} %fusion.3), kind=kOutput, calls=%fused_computation.13 | convolution fusion | flops 17255366656 | bytes 210042880 | tf_op jit(solution)/shard_map/bths,bsc->bthc/dot_general | solution.py:31
  261.1 13.1 %copy.26 = bf16[64,2,64,512]{3,1,0,2:T(2,128)(2,1)} copy(bf16[64,2,64,512]{3,2,1,0:T(8,128)(2,1)} %divide_convert_fusion) | data formatting | bytes 16777216 | tf_op jit(solution)/shard_map/convert_element_type | solution.py:32
  274.3 0.0 all-to-all-done
  274.3 5.8 %all-to-all-start.1 = ((bf16[64,2,64,512]{3,1,0,2:T(2,128)(2,1)}), bf16[64,2,64,512]{3,1,0,2:T(2,128)(2,1)}, u32[]{:S(2)}, u32[]{:S(2)}) async-start(bf16[64,2,64,512]{3,1,0,2:T(2,128)(2,1)} %copy.26), calls=%async_computation.1 | async-start | bytes 16777216 | tf_op jit(solution)/shard_map/all_to_all | solution.py:34
  280.1 0.5 broadcast.65
  280.6 0.7 reduce
  281.4 0.1 reshape.90
  281.6 0.7 copy.25
  282.3 90.6 %all-to-all-done.1 = bf16[64,2,64,512]{3,1,0,2:T(2,128)(2,1)} async-done(((bf16[64,2,64,512]{3,1,0,2:T(2,128)(2,1)}), bf16[64,2,64,512]{3,1,0,2:T(2,128)(2,1)}, u32[]{:S(2)}, u32[]{:S(2)}) %all-to-all-start.1) | async-done | bytes 8388640 | tf_op jit(solution)/shard_map/all_to_all | solution.py:34
  372.9 14.9 %fusion.9 = bf16[64,2,16,512]{3,1,0,2:T(2,128)(2,1)} fusion(bf16[64,2,4,16,512]{4,1,0,3,2:T(2,128)(2,1)} %bitcast.9, f32[64,2,4,16]{1,0,3,2:T(8,128)S(1)} %copy.25), kind=kLoop, calls=%fused_computation.12 | loop fusion | flops 11534336 | bytes 10518528 | tf_op jit(solution)/shard_map/reduce_sum | solution.py:38
  387.8 5.1 %copy.27 = bf16[64,2,16,512]{3,2,1,0:T(8,128)(2,1)} copy(bf16[64,2,16,512]{3,1,0,2:T(2,128)(2,1)} %fusion.9) | data formatting | bytes 4194304 | tf_op jit(solution)/shard_map/convert_element_type | solution.py:39
  (8 shorter events, 0.1 us)
Async XLA Ops:
  6.5 73.0 %all-gather.2.cloned.1.call-start = ((), (), s32[]{:S(2)}) async-start(), calls=%async_computation.2 | async-start | bytes 13107200 | tf_op jit(solution)/shard_map/all_gather | solution.py:21
  192.4 81.8 %all-to-all-start = ((f32[4,1,2048]{2,1,0:T(1,128)}), f32[4,1,2048]{2,1,0:T(1,128)S(1)}, u32[]{:S(2)}, u32[]{:S(2)}) async-start(f32[4,1,2048]{2,1,0:T(1,128)} %reshape.89), calls=%async_computation | async-start | bytes 65536 | tf_op jit(solution)/shard_map/all_to_all | solution.py:35
  274.3 98.6 %all-to-all-start.1 = ((bf16[64,2,64,512]{3,1,0,2:T(2,128)(2,1)}), bf16[64,2,64,512]{3,1,0,2:T(2,128)(2,1)}, u32[]{:S(2)}, u32[]{:S(2)}) async-start(bf16[64,2,64,512]{3,1,0,2:T(2,128)(2,1)} %copy.26), calls=%async_computation.1 | async-start | bytes 16777216 | tf_op jit(solution)/shard_map/all_to_all | solution.py:34
Sparse Core Ops, SparseCore 0:
  8.9 70.6 all-gather.1
where the time goes:
time: 400 us
  waiting for transfers between devices  162 us (40%)
  matrix products  156 us (39%)
  other arithmetic  38.7 us (10%)
  local copies, waits for them, and re-layouts  20.5 us (5%)
  between operations  13.5 us (3%)
  starting transfers between devices  9.11 us (2%)
    all_to_all x1, waiting for transfers between devices, local_step(): lax.all_to_all(part_out, 'dcp', 2, 2, tiled=True)  90.6 us
    dot_general x1, matrix products, local_step(): jnp.einsum('bthd,bsd->bths', q_all, local_keys, preferred_element_type=jn...  90.5 us
    all_gather x1, waiting for transfers between devices, local_step(): q_all = lax.all_gather(q_blk, 'dcp', axis=2, tiled=True)  70.7 us
    dot_general x1, matrix products, local_step(): jnp.einsum('bths,bsc->bthc', weights.astype(jnp.bfloat16), local_keys[:,...  65.4 us
    reduce_sum x1, other arithmetic, local_step(): row_sum = jnp.sum(weights, axis=-1)  21.5 us
    reduce_sum x1, other arithmetic, local_step(): merged = jnp.sum(merge_w[..., None] * recv_out.astype(jnp.float32), axis=2)  14.9 us
    convert_element_type x1, local copies, waits for them, and re-layouts, local_step(): part_out = (part_out / row_sum[..., None]).astype(jnp.bfloat16)  13.1 us
  transfers between devices with their start and end apart: 3, of which 2 were waited for; matrix products, arithmetic and copies ran while one was open for 21% of the time, Pallas kernels for 0%

commit v1 on v0

v1 whole, which is shorter than its diff:
```python
import functools
import math

import jax
import jax.numpy as jnp
from jax import lax
from jax.experimental import pallas as pl
from jax.experimental.pallas import tpu as pltpu
from jax.sharding import PartitionSpec as P

LATENT = 512
ROPE = 64
NOPE = 128
PAGE = 64
MASKED = -1e30
LANES = 128
PAIR = 2
AHEAD = 8
MESH_ID = pl.DeviceIdType.MESH
F32 = jnp.float32
BF16 = jnp.bfloat16


def _nt_dot(a, b):
    return lax.dot_general(a, b, (((1,), (1,)), ((), ())), preferred_element_type=F32)


def _mod2(i):
    return i % 2 if isinstance(i, int) else lax.rem(i, 2)


def _kernel(len_ref, q_hbm, kv_hbm, o_hbm,
            q_own, q_lat, q_rope, kv_buf, s_a, s_b, p_a, p_b,
            keep, part_send, part_recv, mine, mine_lse,
            ici_send, ici_recv, lse_send, lse_recv, out_buf,
            own_sem, kv_sem, qs_sem, qr_sem, part_ssem, part_rsem, ici_ssem, ici_rsem, out_sem):
    batch, toks, heads, width = q_own.shape
    steps = batch // PAIR
    seq_loc = kv_buf.shape[2]
    rows = toks * heads
    tile = LANES
    group = 4
    me = lax.axis_index('dcp')
    core = lax.rem(me, 2)
    partner = me + 1 - 2 * core
    across = lax.rem(me + 2, group)

    barrier = pltpu.get_barrier_semaphore()
    for peer in (partner, across):
        pl.semaphore_signal(barrier, inc=1, device_id={'dcp': peer}, device_id_type=MESH_ID)

    own_copy = pltpu.make_async_copy(q_hbm, q_own, own_sem.at[0])
    own_copy.start()

    def kv_copy(i, s):
        slot = _mod2(i)
        return pltpu.make_async_copy(kv_hbm.at[PAIR * i + s], kv_buf.at[slot, s], kv_sem.at[slot, s])

    for s in range(PAIR):
        kv_copy(0, s).start()

    def pair(i):
        return pl.ds(PAIR * i, PAIR)

    def q_send(i, dest):
        slot = (2, 1, 3)[dest]
        peer = (partner, across, partner)[dest]
        if dest == 2:
            lat_src, rope_src = q_lat.at[pair(i), 1], q_rope.at[pair(i), 1]
        else:
            lat_src, rope_src = q_own.at[pair(i), :, :, pl.ds(0, LATENT)], q_rope.at[pair(i), 0]
        lat = pltpu.make_async_remote_copy(
            src_ref=lat_src, dst_ref=q_lat.at[pair(i), slot],
            send_sem=qs_sem.at[dest, 0, i], recv_sem=qr_sem.at[slot - 1, 0, i],
            device_id={'dcp': peer}, device_id_type=MESH_ID)
        rope = pltpu.make_async_remote_copy(
            src_ref=rope_src, dst_ref=q_rope.at[pair(i), slot],
            send_sem=qs_sem.at[dest, 1, i], recv_sem=qr_sem.at[slot - 1, 1, i],
            device_id={'dcp': peer}, device_id_type=MESH_ID)
        return lat, rope

    def q_start(i, dest):
        for c in q_send(i, dest):
            c.start()

    def q_arrived(i, dest):
        for c in q_send(i, dest):
            c.wait_recv()

    def part_copy(i):
        slot = _mod2(i)
        return pltpu.make_async_remote_copy(
            src_ref=part_send.at[slot], dst_ref=part_recv.at[i],
            send_sem=part_ssem.at[slot], recv_sem=part_rsem.at[i],
            device_id={'dcp': partner}, device_id_type=MESH_ID)

    def ici_copies(i):
        out = pltpu.make_async_remote_copy(
            src_ref=ici_send.at[i], dst_ref=ici_recv.at[i],
            send_sem=ici_ssem.at[0, i], recv_sem=ici_rsem.at[0, i],
            device_id={'dcp': across}, device_id_type=MESH_ID)
        lse = pltpu.make_async_remote_copy(
            src_ref=lse_send.at[i], dst_ref=lse_recv.at[i],
            send_sem=ici_ssem.at[1, i], recv_sem=ici_rsem.at[1, i],
            device_id={'dcp': across}, device_id_type=MESH_ID)
        return out, lse

    def out_copy(i):
        return pltpu.make_async_copy(out_buf.at[pair(i)], o_hbm.at[pair(i)], out_sem.at[i])

    own_copy.wait()

    def pack(b, carry):
        first = q_own[b, 0, :, LATENT:width]
        second = q_own[b, 1, :, LATENT:width]
        q_rope[b, 0] = jnp.concatenate([first, second], axis=-1)
        return carry

    lax.fori_loop(0, batch, pack, 0)
    pl.semaphore_wait(barrier, 2)
    for i in range(AHEAD):
        q_start(i, 1)
        q_start(i, 0)

    scale2 = (NOPE + ROPE) ** -0.5 * math.log2(math.e)
    row_tok = lax.rem(lax.broadcasted_iota(jnp.int32, (group * rows, 1), 0) // heads, toks)
    col = lax.broadcasted_iota(jnp.int32, (1, seq_loc), 1)
    col_pos = (col // PAGE) * (group * PAGE) + lax.rem(col, PAGE) + me * PAGE
    half = lax.broadcasted_iota(jnp.int32, (group * rows // 2, LANES), 1) < LANES // 2

    def load_q(b):
        own = q_own[b, :, :, 0:LATENT].reshape(rows, LATENT)
        others = q_lat[b, 1:4].reshape(3 * rows, LATENT)
        lat = jnp.concatenate([own, others], axis=0)
        packed = q_rope[b]
        first = packed[:, :, 0:ROPE]
        second = packed[:, :, ROPE:2 * ROPE]
        rope = jnp.stack([first, second], axis=1).reshape(group * rows, ROPE)
        return lat, rope

    def scores(i, s, s_ref):
        slot = _mod2(i)
        b = PAIR * i + s
        lat, rope = load_q(b)
        last = len_ref[b] - toks + row_tok
        best = None
        chunk = 512
        for n in range(seq_loc // chunk):
            at = pl.ds(n * chunk, chunk)
            sc = _nt_dot(lat, kv_buf[slot, s, at, 0:LATENT]) + _nt_dot(rope, kv_buf[slot, s, at, LATENT:width])
            sc = jnp.where(col_pos[:, n * chunk:(n + 1) * chunk] <= last, sc * scale2, MASKED)
            s_ref[:, at] = sc
            for t in range(chunk // tile):
                piece = sc[:, t * tile:(t + 1) * tile]
                best = piece if best is None else jnp.maximum(best, piece)
        return jnp.max(best, axis=1, keepdims=True)

    def attend(i, s, s_ref, p_ref, top):
        slot = _mod2(i)
        total = None
        for n in range(seq_loc // tile):
            w = jnp.exp2(s_ref[:, n * tile:(n + 1) * tile] - top)
            total = w if total is None else total + w
            p_ref[:, n * tile:(n + 1) * tile] = w.astype(BF16)
        out = jnp.dot(p_ref[...], kv_buf[slot, s, :, 0:LATENT], preferred_element_type=F32)
        norm = jnp.sum(total, axis=1, keepdims=True)
        stats = jnp.where(half[0:1], top, norm)
        h = group * rows // 2
        keep[slot, s, :, 0:LATENT] = out[:h]
        keep[slot, s, :, LATENT:LATENT + LANES] = stats[:h]
        part_send[slot, s, :, 0:LATENT] = out[h:]
        part_send[slot, s, :, LATENT:LATENT + LANES] = stats[h:]

    row_id = lax.broadcasted_iota(jnp.int32, (rows, LANES), 0)
    lane_id = lax.broadcasted_iota(jnp.int32, (rows, LANES), 1)

    def merge(i):
        slot = _mod2(i)
        lse_row = None
        for s in range(PAIR):
            st_a = keep[slot, s, :, LATENT:LATENT + LANES]
            st_b = part_recv[i, s, :, LATENT:LATENT + LANES]
            m_a, l_a = st_a[:, 0:1], st_a[:, LANES // 2:LANES // 2 + 1]
            m_b, l_b = st_b[:, 0:1], st_b[:, LANES // 2:LANES // 2 + 1]
            m = jnp.maximum(m_a, m_b)
            w_a, w_b = jnp.exp2(m_a - m), jnp.exp2(m_b - m)
            norm = l_a * w_a + l_b * w_b
            lse = m + jnp.log2(norm)
            inv = 1.0 / norm
            both = keep[slot, s, :, 0:LATENT] * (w_a * inv) + part_recv[i, s, :, 0:LATENT] * (w_b * inv)
            mine[i, s] = both[:rows]
            ici_send[i, s] = both[rows:].astype(BF16)
            wide = jnp.broadcast_to(lse, (2 * rows, LANES))
            mine_lse[i, s] = wide[:rows]
            picked = jnp.where(lane_id == row_id + s * rows, wide[rows:], 0.0)
            lse_row = picked if lse_row is None else lse_row + picked
        lse_send[i] = jnp.sum(lse_row, axis=0, keepdims=True)

    def finish(i):
        row = jnp.broadcast_to(lse_recv[i], (rows, LANES))
        for s in range(PAIR):
            lse_b = jnp.sum(jnp.where(lane_id == row_id + s * rows, row, 0.0), axis=1, keepdims=True)
            lse_a = mine_lse[i, s, :, 0:1]
            m = jnp.maximum(lse_a, lse_b)
            w_a, w_b = jnp.exp2(lse_a - m), jnp.exp2(lse_b - m)
            inv = 1.0 / (w_a + w_b)
            o = mine[i, s] * (w_a * inv) + ici_recv[i, s].astype(F32) * (w_b * inv)
            out_buf[PAIR * i + s] = o.astype(BF16).reshape(toks, heads, LATENT)

    def step(i, compute, merging, sending, first=False):
        if sending:
            for c in ici_copies(i - 3):
                c.start()
        if merging:
            part_copy(i - 2).wait()
        if compute or merging:
            if not first:
                if isinstance(i, int) and i - 1 >= steps:
                    pass
                else:
                    part_copy(i - 1).start()
        if compute:
            for s in range(PAIR):
                kv_copy(i, s).wait()

            def prefetch():
                for s in range(PAIR):
                    kv_copy(i + 1, s).start()
                q_arrived(i + 1, 1)
                q_start(i + 1, 2)

            def more():
                q_start(i + AHEAD, 1)
                q_start(i + AHEAD, 0)

            if isinstance(i, int):
                if i + 1 < steps:
                    prefetch()
                if i + AHEAD < steps:
                    more()
            else:
                pl.when(i + AHEAD < steps)(more)
                pl.when(i + 1 < steps)(prefetch)
            q_arrived(i, 0)
            q_arrived(i, 2)
        if merging:
            merge(i - 2)
        if compute:
            tops = [scores(i, 0, s_a), scores(i, 1, s_b)]
            attend(i, 0, s_a, p_a, tops[0])
            attend(i, 1, s_b, p_b, tops[1])

    q_arrived(0, 1)
    q_start(0, 2)
    step(0, True, False, False, first=True)
    step(1, True, False, False)
    step(2, True, True, False)

    def body(i, carry):
        step(i, True, True, True)
        return carry

    lax.fori_loop(3, steps, body, 0)
    step(steps, False, True, True)
    step(steps + 1, False, True, True)
    step(steps + 2, False, False, True)

    def tail(i, carry):
        for c in ici_copies(i):
            c.wait_recv()
        finish(i)
        out_copy(i).start()
        return carry

    lax.fori_loop(0, steps, tail, 0)

    def drain(i, carry):
        out_copy(i).wait()
        for c in ici_copies(i):
            c.wait_send()
        for dest in range(3):
            for c in q_send(i, dest):
                c.wait_send()
        return carry

    lax.fori_loop(0, steps, drain, 0)


def solution(mesh):
    def local_step(q_blk, kv_blk, len_blk):
        batch, toks, heads, width = q_blk.shape
        rounds = kv_blk.shape[1]
        seq_loc = rounds * PAGE
        steps = batch // PAIR
        rows = toks * heads
        keys = kv_blk.reshape(batch, seq_loc, width)
        wide = LATENT + LANES
        dma = pltpu.SemaphoreType.DMA
        return pl.pallas_call(
            _kernel,
            out_shape=jax.ShapeDtypeStruct((batch, toks, heads, LATENT), BF16),
            in_specs=[
                pl.BlockSpec(memory_space=pltpu.SMEM),
                pl.BlockSpec(memory_space=pl.ANY),
                pl.BlockSpec(memory_space=pl.ANY),
            ],
            out_specs=pl.BlockSpec(memory_space=pl.ANY),
            scratch_shapes=[
                pltpu.VMEM((batch, toks, heads, width), BF16),
                pltpu.VMEM((batch, 4, toks, heads, LATENT), BF16),
                pltpu.VMEM((batch, 4, heads, toks * ROPE), BF16),
                pltpu.VMEM((2, PAIR, seq_loc, width), BF16),
                pltpu.VMEM((4 * rows, seq_loc), F32),
                pltpu.VMEM((4 * rows, seq_loc), F32),
                pltpu.VMEM((4 * rows, seq_loc), BF16),
                pltpu.VMEM((4 * rows, seq_loc), BF16),
                pltpu.VMEM((2, PAIR, 2 * rows, wide), F32),
                pltpu.VMEM((2, PAIR, 2 * rows, wide), F32),
                pltpu.VMEM((steps, PAIR, 2 * rows, wide), F32),
                pltpu.VMEM((steps, PAIR, rows, LATENT), F32),
                pltpu.VMEM((steps, PAIR, rows, LANES), F32),
                pltpu.VMEM((steps, PAIR, rows, LATENT), BF16),
                pltpu.VMEM((steps, PAIR, rows, LATENT), BF16),
                pltpu.VMEM((steps, 1, LANES), F32),
                pltpu.VMEM((steps, 1, LANES), F32),
                pltpu.VMEM((batch, toks, heads, LATENT), BF16),
                dma((1,)),
                dma((2, PAIR)),
                dma((3, 2, steps)),
                dma((3, 2, steps)),
                dma((2,)),
                dma((steps,)),
                dma((2, steps)),
                dma((2, steps)),
                dma((steps,)),
            ],
            compiler_params=pltpu.CompilerParams(
                collective_id=0, has_side_effects=True, vmem_limit_bytes=66_000_000),
            name='mla_decode',
        )(len_blk, q_blk, keys)

    return jax.shard_map(
        local_step, mesh=mesh,
        in_specs=(P('dp', None, 'dcp', None), P('dp', None, 'dcp', None, None), P('dp')),
        out_specs=P('dp', None, 'dcp', None), check_vma=False)
```

time: 400 us -> 118 us (0.29)
  waiting for transfers between devices: 162 us -> 0 us
  matrix products: 156 us -> 0 us
  Pallas kernels: 0 us -> 115 us
  other arithmetic: 38.7 us -> 0 us
  local copies, waits for them, and re-layouts: 20.5 us -> 3.22 us
  between operations: 13.5 us -> 0.01 us
  starting transfers between devices: 9.11 us -> 0 us
    dot_general x2 -> x0, matrix products: 156 us -> none  [the longest x1 90.5 us: local_step(): jnp.einsum('bthd,bsd->bths', q_all, local_keys, preferred_element_type=jn...]
    pallas_call x0 -> x1, Pallas kernels: none -> 115 us  [local_step(): pl.pallas_call(_kernel, out_shape=jax.ShapeDtypeStruct((batch, toks, head...]
    all_to_all x2 -> x0, waiting for transfers between devices: 90.6 us -> none  [the longest x1 90.6 us: local_step(): lax.all_to_all(part_out, 'dcp', 2, 2, tiled=True)]
    all_gather x1 -> x0, waiting for transfers between devices: 70.7 us -> none  [local_step(): q_all = lax.all_gather(q_blk, 'dcp', axis=2, tiled=True)]
    reduce_sum x3 -> x0, other arithmetic: 36.4 us -> none  [the longest x1 21.5 us: local_step(): row_sum = jnp.sum(weights, axis=-1)]
    convert_element_type x2 -> x0, local copies, waits for them, and re-layouts: 18.3 us -> none  [the longest x1 13.1 us: local_step(): part_out = (part_out / row_sum[..., None]).astype(jnp.bfloat16)]
    all_to_all x2 -> x0, starting transfers between devices: 9.11 us -> none  [the longest x1 5.85 us: local_step(): lax.all_to_all(part_out, 'dcp', 2, 2, tiled=True)]
  transfers between devices with their start and end apart: 3 -> 0, of which waited for: 2 -> 0; matrix products, arithmetic and copies ran while one was open for 21% -> 0% of each run, Pallas kernels for 0% -> 0%
where the time goes in v1:
time: 118 us
  Pallas kernels  115 us (97%)
  local copies, waits for them, and re-layouts  3.22 us (3%)
    pallas_call x1, Pallas kernels, local_step(): pl.pallas_call(_kernel, out_shape=jax.ShapeDtypeStruct((batch, toks, head...  115 us
    unnamed x1, local copies, waits for them, and re-layouts  3.22 us

profile of v1, /device:TPU:0, one launch (start us, length us, event | category | flops | bytes accessed | tf_op | source)
XLA Modules:
  0.0 118.1 jit_solution(11066306254885963745)
XLA Ops:
  0.0 114.9 %mla_decode.1 = bf16[64,2,16,512]{3,2,1,0:T(8,128)(2,1)} custom-call(s32[64]{0:T(128)} %len_ref.1, bf16[64,2,16,576]{3,2,1,0:T(8,128)(2,1)} %q_hbm.1, bf16[64,2048,576]{2,1,0:T(8,128)(2,1)} %bitcast.kv_hbm), custom_call_target="tpu_custom_call" | custom-call | tf_op jit(solution)/shard_map/mla_decode/pallas_call | solution.py:299
  114.9 3.2 %copy.5 = bf16[64,2,16,512]{3,2,1,0:T(8,128)(2,1)} copy(bf16[64,2,16,512]{3,2,1,0:T(8,128)(2,1)} %mla_decode.1) | data formatting | bytes 4194304

commit v2 on v1

--- a/solution.py
+++ b/solution.py
@@ -16,6 +16,7 @@
 LANES = 128
 PAIR = 2
 AHEAD = 8
+DEPTH = 3
 MESH_ID = pl.DeviceIdType.MESH
 F32 = jnp.float32
 BF16 = jnp.bfloat16
@@ -25,15 +26,15 @@
     return lax.dot_general(a, b, (((1,), (1,)), ((), ())), preferred_element_type=F32)
 
 
-def _mod2(i):
-    return i % 2 if isinstance(i, int) else lax.rem(i, 2)
-
-
-def _kernel(len_ref, q_hbm, kv_hbm, o_hbm,
+def _mod(i, n):
+    return i % n if isinstance(i, int) else lax.rem(i, n)
+
+
+def _kernel(len_ref, q_hbm, kv_hbm, out_buf,
             q_own, q_lat, q_rope, kv_buf, s_a, s_b, p_a, p_b,
             keep, part_send, part_recv, mine, mine_lse,
-            ici_send, ici_recv, lse_send, lse_recv, out_buf,
-            own_sem, kv_sem, qs_sem, qr_sem, part_ssem, part_rsem, ici_ssem, ici_rsem, out_sem):
+            ici_send, ici_recv, lse_send, lse_recv,
+            own_sem, kv_sem, qs_sem, qr_sem, part_ssem, part_rsem, ici_ssem, ici_rsem):
     batch, toks, heads, width = q_own.shape
     steps = batch // PAIR
     seq_loc = kv_buf.shape[2]
@@ -49,15 +50,19 @@
     for peer in (partner, across):
         pl.semaphore_signal(barrier, inc=1, device_id={'dcp': peer}, device_id_type=MESH_ID)
 
-    own_copy = pltpu.make_async_copy(q_hbm, q_own, own_sem.at[0])
-    own_copy.start()
+    early = PAIR * AHEAD
+    own_copies = []
+    for k, (lo, n) in enumerate(((0, early), (early, batch - early))):
+        own_copies.append(pltpu.make_async_copy(q_hbm.at[pl.ds(lo, n)], q_own.at[pl.ds(lo, n)], own_sem.at[k]))
+        own_copies[-1].start()
 
     def kv_copy(i, s):
-        slot = _mod2(i)
+        slot = _mod(i, DEPTH)
         return pltpu.make_async_copy(kv_hbm.at[PAIR * i + s], kv_buf.at[slot, s], kv_sem.at[slot, s])
 
-    for s in range(PAIR):
-        kv_copy(0, s).start()
+    for i in range(DEPTH - 1):
+        for s in range(PAIR):
+            kv_copy(i, s).start()
 
     def pair(i):
         return pl.ds(PAIR * i, PAIR)
@@ -88,7 +93,7 @@
             c.wait_recv()
 
     def part_copy(i):
-        slot = _mod2(i)
+        slot = _mod(i, 2)
         return pltpu.make_async_remote_copy(
             src_ref=part_send.at[slot], dst_ref=part_recv.at[i],
             send_sem=part_ssem.at[slot], recv_sem=part_rsem.at[i],
@@ -105,22 +110,24 @@
             device_id={'dcp': across}, device_id_type=MESH_ID)
         return out, lse
 
-    def out_copy(i):
-        return pltpu.make_async_copy(out_buf.at[pair(i)], o_hbm.at[pair(i)], out_sem.at[i])
-
-    own_copy.wait()
-
-    def pack(b, carry):
-        first = q_own[b, 0, :, LATENT:width]
-        second = q_own[b, 1, :, LATENT:width]
-        q_rope[b, 0] = jnp.concatenate([first, second], axis=-1)
+    unroll = 8
+
+    def pack(k, carry):
+        for u in range(unroll):
+            b = unroll * k + u
+            first = q_own[b, 0, :, LATENT:width]
+            second = q_own[b, 1, :, LATENT:width]
+            q_rope[b, 0] = jnp.concatenate([first, second], axis=-1)
         return carry
 
-    lax.fori_loop(0, batch, pack, 0)
+    own_copies[0].wait()
+    lax.fori_loop(0, early // unroll, pack, 0)
     pl.semaphore_wait(barrier, 2)
     for i in range(AHEAD):
         q_start(i, 1)
         q_start(i, 0)
+    own_copies[1].wait()
+    lax.fori_loop(early // unroll, batch // unroll, pack, 0)
 
     scale2 = (NOPE + ROPE) ** -0.5 * math.log2(math.e)
     row_tok = lax.rem(lax.broadcasted_iota(jnp.int32, (group * rows, 1), 0) // heads, toks)
@@ -139,7 +146,7 @@
         return lat, rope
 
     def scores(i, s, s_ref):
-        slot = _mod2(i)
+        slot = _mod(i, DEPTH)
         b = PAIR * i + s
         lat, rope = load_q(b)
         last = len_ref[b] - toks + row_tok
@@ -156,13 +163,13 @@
         return jnp.max(best, axis=1, keepdims=True)
 
     def attend(i, s, s_ref, p_ref, top):
-        slot = _mod2(i)
+        slot, held = _mod(i, 2), _mod(i, DEPTH)
         total = None
         for n in range(seq_loc // tile):
             w = jnp.exp2(s_ref[:, n * tile:(n + 1) * tile] - top)
             total = w if total is None else total + w
             p_ref[:, n * tile:(n + 1) * tile] = w.astype(BF16)
-        out = jnp.dot(p_ref[...], kv_buf[slot, s, :, 0:LATENT], preferred_element_type=F32)
+        out = jnp.dot(p_ref[...], kv_buf[held, s, :, 0:LATENT], preferred_element_type=F32)
         norm = jnp.sum(total, axis=1, keepdims=True)
         stats = jnp.where(half[0:1], top, norm)
         h = group * rows // 2
@@ -175,7 +182,7 @@
     lane_id = lax.broadcasted_iota(jnp.int32, (rows, LANES), 1)
 
     def merge(i):
-        slot = _mod2(i)
+        slot = _mod(i, 2)
         lse_row = None
         for s in range(PAIR):
             st_a = keep[slot, s, :, LATENT:LATENT + LANES]
@@ -225,7 +232,9 @@
 
             def prefetch():
                 for s in range(PAIR):
-                    kv_copy(i + 1, s).start()
+                    kv_copy(i + DEPTH - 1, s).start()
+
+            def forward():
                 q_arrived(i + 1, 1)
                 q_start(i + 1, 2)
 
@@ -234,13 +243,16 @@
                 q_start(i + AHEAD, 0)
 
             if isinstance(i, int):
-                if i + 1 < steps:
+                if i + DEPTH - 1 < steps:
                     prefetch()
                 if i + AHEAD < steps:
                     more()
+                if i + 1 < steps:
+                    forward()
             else:
+                pl.when(i + DEPTH - 1 < steps)(prefetch)
                 pl.when(i + AHEAD < steps)(more)
-                pl.when(i + 1 < steps)(prefetch)
+                pl.when(i + 1 < steps)(forward)
             q_arrived(i, 0)
             q_arrived(i, 2)
         if merging:
@@ -265,25 +277,24 @@
     step(steps + 1, False, True, True)
     step(steps + 2, False, False, True)
 
-    def tail(i, carry):
-        for c in ici_copies(i):
-            c.wait_recv()
-        finish(i)
-        out_copy(i).start()
-        return carry
-
-    lax.fori_loop(0, steps, tail, 0)
-
-    def drain(i, carry):
-        out_copy(i).wait()
-        for c in ici_copies(i):
-            c.wait_send()
+    def arrive(i):
         for dest in range(3):
             for c in q_send(i, dest):
                 c.wait_send()
+        for c in ici_copies(i):
+            c.wait()
+
+    def tail(k, carry):
+        for u in range(4):
+            arrive(4 * k + u)
+        for u in range(4):
+            finish(4 * k + u)
         return carry
 
-    lax.fori_loop(0, steps, drain, 0)
+    lax.fori_loop(0, steps // 4 - 1, tail, 0)
+    for i in range(steps - 4, steps):
+        arrive(i)
+        finish(i)
 
 
 def solution(mesh):
@@ -298,18 +309,18 @@
         dma = pltpu.SemaphoreType.DMA
         return pl.pallas_call(
             _kernel,
-            out_shape=jax.ShapeDtypeStruct((batch, toks, heads, LATENT), BF16),
+            out_shape=pltpu.VMEM((batch, toks, heads, LATENT), BF16),
             in_specs=[
                 pl.BlockSpec(memory_space=pltpu.SMEM),
                 pl.BlockSpec(memory_space=pl.ANY),
                 pl.BlockSpec(memory_space=pl.ANY),
             ],
-            out_specs=pl.BlockSpec(memory_space=pl.ANY),
+            out_specs=pl.BlockSpec(memory_space=pltpu.VMEM),
             scratch_shapes=[
                 pltpu.VMEM((batch, toks, heads, width), BF16),
                 pltpu.VMEM((batch, 4, toks, heads, LATENT), BF16),
                 pltpu.VMEM((batch, 4, heads, toks * ROPE), BF16),
-                pltpu.VMEM((2, PAIR, seq_loc, width), BF16),
+                pltpu.VMEM((DEPTH, PAIR, seq_loc, width), BF16),
                 pltpu.VMEM((4 * rows, seq_loc), F32),
                 pltpu.VMEM((4 * rows, seq_loc), F32),
                 pltpu.VMEM((4 * rows, seq_loc), BF16),
@@ -323,19 +334,17 @@
                 pltpu.VMEM((steps, PAIR, rows, LATENT), BF16),
                 pltpu.VMEM((steps, 1, LANES), F32),
                 pltpu.VMEM((steps, 1, LANES), F32),
-                pltpu.VMEM((batch, toks, heads, LATENT), BF16),
-                dma((1,)),
-                dma((2, PAIR)),
+                dma((2,)),
+                dma((DEPTH, PAIR)),
                 dma((3, 2, steps)),
                 dma((3, 2, steps)),
                 dma((2,)),
                 dma((steps,)),
                 dma((2, steps)),
                 dma((2, steps)),
-                dma((steps,)),
             ],
             compiler_params=pltpu.CompilerParams(
-                collective_id=0, has_side_effects=True, vmem_limit_bytes=66_000_000),
+                collective_id=0, has_side_effects=True, vmem_limit_bytes=60_000_000),
             name='mla_decode',
         )(len_blk, q_blk, keys)
 

time: 118 us -> 111 us (0.941)
  Pallas kernels: 115 us -> 109 us
  local copies, waits for them, and re-layouts: 3.22 us -> 1.32 us
    pallas_call x1, Pallas kernels: 115 us -> 109 us  [local_step(): pl.pallas_call(_kernel, out_shape=pltpu.VMEM((batch, toks, heads, LATENT)...]
    unnamed x1, local copies, waits for them, and re-layouts: 3.22 us -> 1.32 us
where the time goes in v2:
time: 111 us; the launch traced here: 110 us
  Pallas kernels  109 us (98%)
  local copies, waits for them, and re-layouts  1.32 us (1%)
    pallas_call x1, Pallas kernels, local_step(): pl.pallas_call(_kernel, out_shape=pltpu.VMEM((batch, toks, heads, LATENT)...  109 us

profile of v2, /device:TPU:0, one launch (start us, length us, event | category | flops | bytes accessed | tf_op | source)
XLA Modules:
  0.0 110.4 jit_solution(15841346827487249093)
XLA Ops:
  0.0 109.1 %mla_decode.1 = bf16[64,2,16,512]{3,2,1,0:T(8,128)(2,1)S(1)} custom-call(s32[64]{0:T(128)} %len_ref.1, bf16[64,2,16,576]{3,2,1,0:T(8,128)(2,1)} %q_hbm.1, bf16[64,2048,576]{2,1,0:T(8,128)(2,1)} %bitcast.kv_hbm), custom_call_target="tpu_custom_call" | custom-call | tf_op jit(solution)/shard_map/mla_decode/pallas_call | solution.py:310
  109.1 1.3 %copy.5 = bf16[64,2,16,512]{3,2,1,0:T(8,128)(2,1)} copy(bf16[64,2,16,512]{3,2,1,0:T(8,128)(2,1)S(1)} %mla_decode.1) | data formatting | bytes 4194304

commit v3 on v2

--- a/solution.py
+++ b/solution.py
@@ -15,7 +15,9 @@
 MASKED = -1e30
 LANES = 128
 PAIR = 2
+FIRST = 2
 AHEAD = 8
+LSE_STEPS = 4
 DEPTH = 3
 MESH_ID = pl.DeviceIdType.MESH
 F32 = jnp.float32
@@ -31,7 +33,7 @@
 
 
 def _kernel(len_ref, q_hbm, kv_hbm, out_buf,
-            q_own, q_lat, q_rope, kv_buf, s_a, s_b, p_a, p_b,
+            q_own, q_msg, kv_buf, s_a, s_b, p_a, p_b,
             keep, part_send, part_recv, mine, mine_lse,
             ici_send, ici_recv, lse_send, lse_recv,
             own_sem, kv_sem, qs_sem, qr_sem, part_ssem, part_rsem, ici_ssem, ici_rsem):
@@ -50,47 +52,26 @@
     for peer in (partner, across):
         pl.semaphore_signal(barrier, inc=1, device_id={'dcp': peer}, device_id_type=MESH_ID)
 
-    early = PAIR * AHEAD
+    cuts = (0, PAIR * FIRST, PAIR * AHEAD, batch)
     own_copies = []
-    for k, (lo, n) in enumerate(((0, early), (early, batch - early))):
-        own_copies.append(pltpu.make_async_copy(q_hbm.at[pl.ds(lo, n)], q_own.at[pl.ds(lo, n)], own_sem.at[k]))
+    for k in range(3):
+        at = pl.ds(cuts[k], cuts[k + 1] - cuts[k])
+        own_copies.append(pltpu.make_async_copy(q_hbm.at[at], q_own.at[at], own_sem.at[k]))
         own_copies[-1].start()
 
     def kv_copy(i, s):
         slot = _mod(i, DEPTH)
         return pltpu.make_async_copy(kv_hbm.at[PAIR * i + s], kv_buf.at[slot, s], kv_sem.at[slot, s])
 
-    for i in range(DEPTH - 1):
-        for s in range(PAIR):
-            kv_copy(i, s).start()
-
     def pair(i):
         return pl.ds(PAIR * i, PAIR)
 
     def q_send(i, dest):
         slot = (2, 1, 3)[dest]
-        peer = (partner, across, partner)[dest]
-        if dest == 2:
-            lat_src, rope_src = q_lat.at[pair(i), 1], q_rope.at[pair(i), 1]
-        else:
-            lat_src, rope_src = q_own.at[pair(i), :, :, pl.ds(0, LATENT)], q_rope.at[pair(i), 0]
-        lat = pltpu.make_async_remote_copy(
-            src_ref=lat_src, dst_ref=q_lat.at[pair(i), slot],
-            send_sem=qs_sem.at[dest, 0, i], recv_sem=qr_sem.at[slot - 1, 0, i],
-            device_id={'dcp': peer}, device_id_type=MESH_ID)
-        rope = pltpu.make_async_remote_copy(
-            src_ref=rope_src, dst_ref=q_rope.at[pair(i), slot],
-            send_sem=qs_sem.at[dest, 1, i], recv_sem=qr_sem.at[slot - 1, 1, i],
-            device_id={'dcp': peer}, device_id_type=MESH_ID)
-        return lat, rope
-
-    def q_start(i, dest):
-        for c in q_send(i, dest):
-            c.start()
-
-    def q_arrived(i, dest):
-        for c in q_send(i, dest):
-            c.wait_recv()
+        return pltpu.make_async_remote_copy(
+            src_ref=q_msg.at[1 if dest == 2 else 0, pair(i)], dst_ref=q_msg.at[slot, pair(i)],
+            send_sem=qs_sem.at[dest, i], recv_sem=qr_sem.at[slot - 1, i],
+            device_id={'dcp': (partner, across, partner)[dest]}, device_id_type=MESH_ID)
 
     def part_copy(i):
         slot = _mod(i, 2)
@@ -99,35 +80,51 @@
             send_sem=part_ssem.at[slot], recv_sem=part_rsem.at[i],
             device_id={'dcp': partner}, device_id_type=MESH_ID)
 
-    def ici_copies(i):
-        out = pltpu.make_async_remote_copy(
+    def out_send(i):
+        return pltpu.make_async_remote_copy(
             src_ref=ici_send.at[i], dst_ref=ici_recv.at[i],
             send_sem=ici_ssem.at[0, i], recv_sem=ici_rsem.at[0, i],
             device_id={'dcp': across}, device_id_type=MESH_ID)
-        lse = pltpu.make_async_remote_copy(
-            src_ref=lse_send.at[i], dst_ref=lse_recv.at[i],
-            send_sem=ici_ssem.at[1, i], recv_sem=ici_rsem.at[1, i],
+
+    def lse_row(i):
+        if isinstance(i, int) and i == steps - 1:
+            return steps // LSE_STEPS, 0
+        return i // LSE_STEPS, _mod(i, LSE_STEPS)
+
+    def lse_send_copy(k):
+        return pltpu.make_async_remote_copy(
+            src_ref=lse_send.at[k], dst_ref=lse_recv.at[k],
+            send_sem=ici_ssem.at[1, k], recv_sem=ici_rsem.at[1, k],
             device_id={'dcp': across}, device_id_type=MESH_ID)
-        return out, lse
-
-    unroll = 8
+
+    unroll = PAIR * FIRST
+    lat_tiles = LATENT // LANES
 
     def pack(k, carry):
         for u in range(unroll):
             b = unroll * k + u
-            first = q_own[b, 0, :, LATENT:width]
-            second = q_own[b, 1, :, LATENT:width]
-            q_rope[b, 0] = jnp.concatenate([first, second], axis=-1)
+            for t in range(toks):
+                for n in range(lat_tiles):
+                    q_msg[0, b, t * lat_tiles + n] = q_own[b, t, :, n * LANES:(n + 1) * LANES]
+            q_msg[0, b, toks * lat_tiles] = jnp.concatenate(
+                [q_own[b, t, :, LATENT:width] for t in range(toks)], axis=-1)
         return carry
 
     own_copies[0].wait()
-    lax.fori_loop(0, early // unroll, pack, 0)
+    pack(0, 0)
     pl.semaphore_wait(barrier, 2)
-    for i in range(AHEAD):
-        q_start(i, 1)
-        q_start(i, 0)
-    own_copies[1].wait()
-    lax.fori_loop(early // unroll, batch // unroll, pack, 0)
+    for k in range(2):
+        if k == 1:
+            own_copies[1].wait()
+            lax.fori_loop(1, cuts[2] // unroll, pack, 0)
+        for i in range(cuts[k] // PAIR, cuts[k + 1] // PAIR):
+            q_send(i, 1).start()
+            q_send(i, 0).start()
+    for i in range(DEPTH - 1):
+        for s in range(PAIR):
+            kv_copy(i, s).start()
+    own_copies[2].wait()
+    lax.fori_loop(cuts[2] // unroll, batch // unroll, pack, 0)
 
     scale2 = (NOPE + ROPE) ** -0.5 * math.log2(math.e)
     row_tok = lax.rem(lax.broadcasted_iota(jnp.int32, (group * rows, 1), 0) // heads, toks)
@@ -136,13 +133,12 @@
     half = lax.broadcasted_iota(jnp.int32, (group * rows // 2, LANES), 1) < LANES // 2
 
     def load_q(b):
-        own = q_own[b, :, :, 0:LATENT].reshape(rows, LATENT)
-        others = q_lat[b, 1:4].reshape(3 * rows, LATENT)
-        lat = jnp.concatenate([own, others], axis=0)
-        packed = q_rope[b]
-        first = packed[:, :, 0:ROPE]
-        second = packed[:, :, ROPE:2 * ROPE]
-        rope = jnp.stack([first, second], axis=1).reshape(group * rows, ROPE)
+        lat = jnp.concatenate(
+            [jnp.concatenate([q_msg[g, b, t * lat_tiles + n] for n in range(lat_tiles)], axis=1)
+             for g in range(group) for t in range(toks)], axis=0)
+        rope = jnp.concatenate(
+            [q_msg[g, b, toks * lat_tiles][:, t * ROPE:(t + 1) * ROPE]
+             for g in range(group) for t in range(toks)], axis=0)
         return lat, rope
 
     def scores(i, s, s_ref):
@@ -183,7 +179,7 @@
 
     def merge(i):
         slot = _mod(i, 2)
-        lse_row = None
+        lse_sum = None
         for s in range(PAIR):
             st_a = keep[slot, s, :, LATENT:LATENT + LANES]
             st_b = part_recv[i, s, :, LATENT:LATENT + LANES]
@@ -200,11 +196,13 @@
             wide = jnp.broadcast_to(lse, (2 * rows, LANES))
             mine_lse[i, s] = wide[:rows]
             picked = jnp.where(lane_id == row_id + s * rows, wide[rows:], 0.0)
-            lse_row = picked if lse_row is None else lse_row + picked
-        lse_send[i] = jnp.sum(lse_row, axis=0, keepdims=True)
+            lse_sum = picked if lse_sum is None else lse_sum + picked
+        k, r = lse_row(i)
+        lse_send[k, pl.ds(r, 1)] = jnp.sum(lse_sum, axis=0, keepdims=True)
 
     def finish(i):
-        row = jnp.broadcast_to(lse_recv[i], (rows, LANES))
+        k, r = lse_row(i)
+        row = jnp.broadcast_to(lse_recv[k, pl.ds(r, 1)], (rows, LANES))
         for s in range(PAIR):
             lse_b = jnp.sum(jnp.where(lane_id == row_id + s * rows, row, 0.0), axis=1, keepdims=True)
             lse_a = mine_lse[i, s, :, 0:1]
@@ -216,8 +214,16 @@
 
     def step(i, compute, merging, sending, first=False):
         if sending:
-            for c in ici_copies(i - 3):
-                c.start()
+            out_send(i - 3).start()
+
+            def send_lse():
+                lse_send_copy((i - 2) // LSE_STEPS - 1).start()
+
+            if isinstance(i, int):
+                if i > steps:
+                    lse_send_copy(steps // LSE_STEPS + i - steps - 2).start()
+            else:
+                pl.when(lax.rem(i - 2, LSE_STEPS) == 0)(send_lse)
         if merging:
             part_copy(i - 2).wait()
         if compute or merging:
@@ -235,12 +241,12 @@
                     kv_copy(i + DEPTH - 1, s).start()
 
             def forward():
-                q_arrived(i + 1, 1)
-                q_start(i + 1, 2)
+                q_send(i + 1, 1).wait_recv()
+                q_send(i + 1, 2).start()
 
             def more():
-                q_start(i + AHEAD, 1)
-                q_start(i + AHEAD, 0)
+                q_send(i + AHEAD, 1).start()
+                q_send(i + AHEAD, 0).start()
 
             if isinstance(i, int):
                 if i + DEPTH - 1 < steps:
@@ -253,8 +259,8 @@
                 pl.when(i + DEPTH - 1 < steps)(prefetch)
                 pl.when(i + AHEAD < steps)(more)
                 pl.when(i + 1 < steps)(forward)
-            q_arrived(i, 0)
-            q_arrived(i, 2)
+            q_send(i, 0).wait_recv()
+            q_send(i, 2).wait_recv()
         if merging:
             merge(i - 2)
         if compute:
@@ -262,8 +268,8 @@
             attend(i, 0, s_a, p_a, tops[0])
             attend(i, 1, s_b, p_b, tops[1])
 
-    q_arrived(0, 1)
-    q_start(0, 2)
+    q_send(0, 1).wait_recv()
+    q_send(0, 2).start()
     step(0, True, False, False, first=True)
     step(1, True, False, False)
     step(2, True, True, False)
@@ -279,22 +285,27 @@
 
     def arrive(i):
         for dest in range(3):
-            for c in q_send(i, dest):
-                c.wait_send()
-        for c in ici_copies(i):
-            c.wait()
+            q_send(i, dest).wait_send()
+        out_send(i).wait()
 
     def tail(k, carry):
-        for u in range(4):
-            arrive(4 * k + u)
-        for u in range(4):
-            finish(4 * k + u)
+        for u in range(LSE_STEPS):
+            arrive(LSE_STEPS * k + u)
+        lse_send_copy(k).wait()
+        for u in range(LSE_STEPS):
+            finish(LSE_STEPS * k + u)
         return carry
 
-    lax.fori_loop(0, steps // 4 - 1, tail, 0)
-    for i in range(steps - 4, steps):
+    groups = steps // LSE_STEPS
+    lax.fori_loop(0, groups - 1, tail, 0)
+    for i in range(steps - LSE_STEPS, steps - 1):
         arrive(i)
+    lse_send_copy(groups - 1).wait()
+    for i in range(steps - LSE_STEPS, steps - 1):
         finish(i)
+    arrive(steps - 1)
+    lse_send_copy(groups).wait()
+    finish(steps - 1)
 
 
 def solution(mesh):
@@ -318,8 +329,7 @@
             out_specs=pl.BlockSpec(memory_space=pltpu.VMEM),
             scratch_shapes=[
                 pltpu.VMEM((batch, toks, heads, width), BF16),
-                pltpu.VMEM((batch, 4, toks, heads, LATENT), BF16),
-                pltpu.VMEM((batch, 4, heads, toks * ROPE), BF16),
+                pltpu.VMEM((4, batch, toks * width // LANES, heads, LANES), BF16),
                 pltpu.VMEM((DEPTH, PAIR, seq_loc, width), BF16),
                 pltpu.VMEM((4 * rows, seq_loc), F32),
                 pltpu.VMEM((4 * rows, seq_loc), F32),
@@ -332,12 +342,12 @@
                 pltpu.VMEM((steps, PAIR, rows, LANES), F32),
                 pltpu.VMEM((steps, PAIR, rows, LATENT), BF16),
                 pltpu.VMEM((steps, PAIR, rows, LATENT), BF16),
-                pltpu.VMEM((steps, 1, LANES), F32),
-                pltpu.VMEM((steps, 1, LANES), F32),
-                dma((2,)),
+                pltpu.VMEM((steps // LSE_STEPS + 1, LSE_STEPS, LANES), F32),
+                pltpu.VMEM((steps // LSE_STEPS + 1, LSE_STEPS, LANES), F32),
+                dma((3,)),
                 dma((DEPTH, PAIR)),
-                dma((3, 2, steps)),
-                dma((3, 2, steps)),
+                dma((3, steps)),
+                dma((3, steps)),
                 dma((2,)),
                 dma((steps,)),
                 dma((2, steps)),

time: 111 us -> 107 us (0.964)
  Pallas kernels: 109 us -> 105 us
    pallas_call x1, Pallas kernels: 109 us -> 105 us  [local_step(): pl.pallas_call(_kernel, out_shape=pltpu.VMEM((batch, toks, heads, LATENT)...]
where the time goes in v3:
time: 107 us; the launch traced here: 106 us
  Pallas kernels  105 us (98%)
  local copies, waits for them, and re-layouts  1.32 us (1%)
    pallas_call x1, Pallas kernels, local_step(): pl.pallas_call(_kernel, out_shape=pltpu.VMEM((batch, toks, heads, LATENT)...  105 us

profile of v3, /device:TPU:0, one launch (start us, length us, event | category | flops | bytes accessed | tf_op | source)
XLA Modules:
  0.0 106.4 jit_solution(13913841601537267064)
XLA Ops:
  0.0 105.1 %mla_decode.1 = bf16[64,2,16,512]{3,2,1,0:T(8,128)(2,1)S(1)} custom-call(s32[64]{0:T(128)} %len_ref.1, bf16[64,2,16,576]{3,2,1,0:T(8,128)(2,1)} %q_hbm.1, bf16[64,2048,576]{2,1,0:T(8,128)(2,1)} %bitcast.kv_hbm), custom_call_target="tpu_custom_call" | custom-call | tf_op jit(solution)/shard_map/mla_decode/pallas_call | solution.py:321
  105.1 1.3 %copy.5 = bf16[64,2,16,512]{3,2,1,0:T(8,128)(2,1)} copy(bf16[64,2,16,512]{3,2,1,0:T(8,128)(2,1)S(1)} %mla_decode.1) | data formatting | bytes 4194304

commit v4 on v3

--- a/solution.py
+++ b/solution.py
@@ -32,8 +32,8 @@
     return i % n if isinstance(i, int) else lax.rem(i, n)
 
 
-def _kernel(len_ref, q_hbm, kv_hbm, out_buf,
-            q_own, q_msg, kv_buf, s_a, s_b, p_a, p_b,
+def _kernel(len_hbm, q_hbm, kv_hbm, out_buf,
+            len_ref, q_own, q_msg, kv_buf, s_a, s_b, p_a, p_b,
             keep, part_send, part_recv, mine, mine_lse,
             ici_send, ici_recv, lse_send, lse_recv,
             own_sem, kv_sem, qs_sem, qr_sem, part_ssem, part_rsem, ici_ssem, ici_rsem):
@@ -59,6 +59,9 @@
         own_copies.append(pltpu.make_async_copy(q_hbm.at[at], q_own.at[at], own_sem.at[k]))
         own_copies[-1].start()
 
+    len_copy = pltpu.make_async_copy(len_hbm, len_ref, own_sem.at[3])
+    len_copy.start()
+
     def kv_copy(i, s):
         slot = _mod(i, DEPTH)
         return pltpu.make_async_copy(kv_hbm.at[PAIR * i + s], kv_buf.at[slot, s], kv_sem.at[slot, s])
@@ -66,11 +69,17 @@
     def pair(i):
         return pl.ds(PAIR * i, PAIR)
 
-    def q_send(i, dest):
+    q_msgs = steps // 2 + 1
+
+    def q_send(m, dest):
         slot = (2, 1, 3)[dest]
+        if isinstance(m, int) and m < 2:
+            at = pl.ds(PAIR * m, PAIR)
+        else:
+            at = pl.ds(2 * PAIR * (m - 1), 2 * PAIR)
         return pltpu.make_async_remote_copy(
-            src_ref=q_msg.at[1 if dest == 2 else 0, pair(i)], dst_ref=q_msg.at[slot, pair(i)],
-            send_sem=qs_sem.at[dest, i], recv_sem=qr_sem.at[slot - 1, i],
+            src_ref=q_msg.at[1 if dest == 2 else 0, at], dst_ref=q_msg.at[slot, at],
+            send_sem=qs_sem.at[dest, m], recv_sem=qr_sem.at[slot - 1, m],
             device_id={'dcp': (partner, across, partner)[dest]}, device_id_type=MESH_ID)
 
     def part_copy(i):
@@ -80,16 +89,24 @@
             send_sem=part_ssem.at[slot], recv_sem=part_rsem.at[i],
             device_id={'dcp': partner}, device_id_type=MESH_ID)
 
-    def out_send(i):
+    out_msgs = steps // 2 + 1
+
+    def out_send(m):
+        if isinstance(m, int) and m >= out_msgs - 2:
+            at = pl.ds(m + steps - out_msgs, 1)
+        else:
+            at = pl.ds(2 * m, 2)
         return pltpu.make_async_remote_copy(
-            src_ref=ici_send.at[i], dst_ref=ici_recv.at[i],
-            send_sem=ici_ssem.at[0, i], recv_sem=ici_rsem.at[0, i],
+            src_ref=ici_send.at[at], dst_ref=ici_recv.at[at],
+            send_sem=ici_ssem.at[0, m], recv_sem=ici_rsem.at[0, m],
             device_id={'dcp': across}, device_id_type=MESH_ID)
+
+    groups = steps // LSE_STEPS
 
     def lse_row(i):
         if isinstance(i, int) and i == steps - 1:
-            return steps // LSE_STEPS, 0
-        return i // LSE_STEPS, _mod(i, LSE_STEPS)
+            return groups, 0
+        return i // LSE_STEPS, _mod(i, LSE_STEPS) // 2
 
     def lse_send_copy(k):
         return pltpu.make_async_remote_copy(
@@ -117,12 +134,13 @@
         if k == 1:
             own_copies[1].wait()
             lax.fori_loop(1, cuts[2] // unroll, pack, 0)
-        for i in range(cuts[k] // PAIR, cuts[k + 1] // PAIR):
-            q_send(i, 1).start()
-            q_send(i, 0).start()
+        for m in ((0, 1), range(2, AHEAD // 2 + 1))[k]:
+            q_send(m, 1).start()
+            q_send(m, 0).start()
     for i in range(DEPTH - 1):
         for s in range(PAIR):
             kv_copy(i, s).start()
+    len_copy.wait()
     own_copies[2].wait()
     lax.fori_loop(cuts[2] // unroll, batch // unroll, pack, 0)
 
@@ -195,16 +213,19 @@
             ici_send[i, s] = both[rows:].astype(BF16)
             wide = jnp.broadcast_to(lse, (2 * rows, LANES))
             mine_lse[i, s] = wide[:rows]
-            picked = jnp.where(lane_id == row_id + s * rows, wide[rows:], 0.0)
+            picked = jnp.where(lane_id == row_id + (s * rows + PAIR * rows * _mod(i, 2)), wide[rows:], 0.0)
             lse_sum = picked if lse_sum is None else lse_sum + picked
         k, r = lse_row(i)
-        lse_send[k, pl.ds(r, 1)] = jnp.sum(lse_sum, axis=0, keepdims=True)
+        line = jnp.sum(lse_sum, axis=0, keepdims=True)
+        before = lse_send[k, pl.ds(r, 1)]
+        lse_send[k, pl.ds(r, 1)] = jnp.where(lane_id[0:1] // (PAIR * rows) == _mod(i, 2), line, before)
 
     def finish(i):
         k, r = lse_row(i)
         row = jnp.broadcast_to(lse_recv[k, pl.ds(r, 1)], (rows, LANES))
         for s in range(PAIR):
-            lse_b = jnp.sum(jnp.where(lane_id == row_id + s * rows, row, 0.0), axis=1, keepdims=True)
+            lane = row_id + (s * rows + PAIR * rows * _mod(i, 2))
+            lse_b = jnp.sum(jnp.where(lane_id == lane, row, 0.0), axis=1, keepdims=True)
             lse_a = mine_lse[i, s, :, 0:1]
             m = jnp.maximum(lse_a, lse_b)
             w_a, w_b = jnp.exp2(lse_a - m), jnp.exp2(lse_b - m)
@@ -212,26 +233,18 @@
             o = mine[i, s] * (w_a * inv) + ici_recv[i, s].astype(F32) * (w_b * inv)
             out_buf[PAIR * i + s] = o.astype(BF16).reshape(toks, heads, LATENT)
 
-    def step(i, compute, merging, sending, first=False):
-        if sending:
-            out_send(i - 3).start()
-
-            def send_lse():
-                lse_send_copy((i - 2) // LSE_STEPS - 1).start()
-
-            if isinstance(i, int):
-                if i > steps:
-                    lse_send_copy(steps // LSE_STEPS + i - steps - 2).start()
-            else:
-                pl.when(lax.rem(i - 2, LSE_STEPS) == 0)(send_lse)
+    def when(i, parity, limit, action):
+        if isinstance(i, int):
+            if i % 2 == parity and i < limit:
+                action()
+        else:
+            pl.when(jnp.logical_and(lax.rem(i, 2) == parity, i < limit))(action)
+
+    def step(i, compute=True, merging=True):
         if merging:
             part_copy(i - 2).wait()
-        if compute or merging:
-            if not first:
-                if isinstance(i, int) and i - 1 >= steps:
-                    pass
-                else:
-                    part_copy(i - 1).start()
+        if not (isinstance(i, int) and i == 0):
+            part_copy(i - 1).start()
         if compute:
             for s in range(PAIR):
                 kv_copy(i, s).wait()
@@ -240,27 +253,36 @@
                 for s in range(PAIR):
                     kv_copy(i + DEPTH - 1, s).start()
 
+            def more():
+                m = (i + AHEAD) // 2 + 1
+                q_send(m, 1).start()
+                q_send(m, 0).start()
+
             def forward():
-                q_send(i + 1, 1).wait_recv()
-                q_send(i + 1, 2).start()
-
-            def more():
-                q_send(i + AHEAD, 1).start()
-                q_send(i + AHEAD, 0).start()
+                m = (i + 1) // 2 + 1
+                q_send(m, 1).wait_recv()
+                q_send(m, 2).start()
+
+            def arrived():
+                q_send(i // 2 + 1, 0).wait_recv()
+                q_send(i // 2 + 1, 2).wait_recv()
 
             if isinstance(i, int):
                 if i + DEPTH - 1 < steps:
                     prefetch()
-                if i + AHEAD < steps:
-                    more()
-                if i + 1 < steps:
-                    forward()
             else:
                 pl.when(i + DEPTH - 1 < steps)(prefetch)
-                pl.when(i + AHEAD < steps)(more)
-                pl.when(i + 1 < steps)(forward)
-            q_send(i, 0).wait_recv()
-            q_send(i, 2).wait_recv()
+            when(i, 0, steps - AHEAD, more)
+            if isinstance(i, int) and i == 0:
+                q_send(1, 1).wait_recv()
+                q_send(1, 2).start()
+            else:
+                when(i, 1, steps - 1, forward)
+            if isinstance(i, int) and i < 2:
+                for dest in (0, 2):
+                    q_send(i, dest).wait_recv()
+            else:
+                when(i, 0, steps, arrived)
         if merging:
             merge(i - 2)
         if compute:
@@ -268,43 +290,67 @@
             attend(i, 0, s_a, p_a, tops[0])
             attend(i, 1, s_b, p_b, tops[1])
 
+    def send_out(i):
+        out_send(i // 2 - 2).start()
+
+        def send_lse():
+            lse_send_copy((i - 2) // LSE_STEPS - 1).start()
+
+        if isinstance(i, int):
+            if (i - 2) % LSE_STEPS == 0:
+                send_lse()
+        else:
+            pl.when(lax.rem(i - 2, LSE_STEPS) == 0)(send_lse)
+
     q_send(0, 1).wait_recv()
     q_send(0, 2).start()
-    step(0, True, False, False, first=True)
-    step(1, True, False, False)
-    step(2, True, True, False)
+    step(0, merging=False)
+    step(1, merging=False)
+    step(2)
 
     def body(i, carry):
-        step(i, True, True, True)
+        when(i, 0, steps, lambda: send_out(i))
+        step(i)
         return carry
 
     lax.fori_loop(3, steps, body, 0)
-    step(steps, False, True, True)
-    step(steps + 1, False, True, True)
-    step(steps + 2, False, False, True)
-
-    def arrive(i):
+    send_out(steps)
+    step(steps, compute=False)
+    part_copy(steps - 1).wait()
+    merge(steps - 1)
+    lse_send_copy(groups - 1).start()
+    out_send(out_msgs - 2).start()
+    lse_send_copy(groups).start()
+    out_send(out_msgs - 1).start()
+
+    for dest in range(3):
+        for m in range(2):
+            q_send(m, dest).wait_send()
+
+    def q_sent(m, carry):
         for dest in range(3):
-            q_send(i, dest).wait_send()
-        out_send(i).wait()
+            q_send(m, dest).wait_send()
+        return carry
+
+    lax.fori_loop(2, q_msgs, q_sent, 0)
 
     def tail(k, carry):
-        for u in range(LSE_STEPS):
-            arrive(LSE_STEPS * k + u)
+        for u in range(LSE_STEPS // 2):
+            out_send(LSE_STEPS // 2 * k + u).wait()
         lse_send_copy(k).wait()
         for u in range(LSE_STEPS):
             finish(LSE_STEPS * k + u)
         return carry
 
-    groups = steps // LSE_STEPS
     lax.fori_loop(0, groups - 1, tail, 0)
-    for i in range(steps - LSE_STEPS, steps - 1):
-        arrive(i)
+    out_send(out_msgs - 3).wait()
     lse_send_copy(groups - 1).wait()
-    for i in range(steps - LSE_STEPS, steps - 1):
+    for i in range(steps - LSE_STEPS, steps - 2):
         finish(i)
-    arrive(steps - 1)
+    out_send(out_msgs - 2).wait()
+    finish(steps - 2)
     lse_send_copy(groups).wait()
+    out_send(out_msgs - 1).wait()
     finish(steps - 1)
 
 
@@ -322,12 +368,13 @@
             _kernel,
             out_shape=pltpu.VMEM((batch, toks, heads, LATENT), BF16),
             in_specs=[
-                pl.BlockSpec(memory_space=pltpu.SMEM),
+                pl.BlockSpec(memory_space=pl.ANY),
                 pl.BlockSpec(memory_space=pl.ANY),
                 pl.BlockSpec(memory_space=pl.ANY),
             ],
             out_specs=pl.BlockSpec(memory_space=pltpu.VMEM),
             scratch_shapes=[
+                pltpu.SMEM((batch,), jnp.int32),
                 pltpu.VMEM((batch, toks, heads, width), BF16),
                 pltpu.VMEM((4, batch, toks * width // LANES, heads, LANES), BF16),
                 pltpu.VMEM((DEPTH, PAIR, seq_loc, width), BF16),
@@ -342,16 +389,16 @@
                 pltpu.VMEM((steps, PAIR, rows, LANES), F32),
                 pltpu.VMEM((steps, PAIR, rows, LATENT), BF16),
                 pltpu.VMEM((steps, PAIR, rows, LATENT), BF16),
-                pltpu.VMEM((steps // LSE_STEPS + 1, LSE_STEPS, LANES), F32),
-                pltpu.VMEM((steps // LSE_STEPS + 1, LSE_STEPS, LANES), F32),
-                dma((3,)),
+                pltpu.VMEM((steps // LSE_STEPS + 1, LSE_STEPS // 2, LANES), F32),
+                pltpu.VMEM((steps // LSE_STEPS + 1, LSE_STEPS // 2, LANES), F32),
+                dma((4,)),
                 dma((DEPTH, PAIR)),
-                dma((3, steps)),
-                dma((3, steps)),
+                dma((3, steps // 2 + 1)),
+                dma((3, steps // 2 + 1)),
                 dma((2,)),
                 dma((steps,)),
-                dma((2, steps)),
-                dma((2, steps)),
+                dma((2, steps // 2 + 1)),
+                dma((2, steps // 2 + 1)),
             ],
             compiler_params=pltpu.CompilerParams(
                 collective_id=0, has_side_effects=True, vmem_limit_bytes=60_000_000),

time: 107 us -> 104 us (0.972)
  Pallas kernels: 105 us -> 103 us
    pallas_call x1, Pallas kernels: 105 us -> 103 us  [local_step(): pl.pallas_call(_kernel, out_shape=pltpu.VMEM((batch, toks, heads, LATENT)...]
where the time goes in v4:
time: 104 us
  Pallas kernels  103 us (99%)
  local copies, waits for them, and re-layouts  1.32 us (1%)
    pallas_call x1, Pallas kernels, local_step(): pl.pallas_call(_kernel, out_shape=pltpu.VMEM((batch, toks, heads, LATENT)...  103 us

profile of v4, /device:TPU:0, one launch (start us, length us, event | category | flops | bytes accessed | tf_op | source)
XLA Modules:
  0.0 104.2 jit_solution(5458220396990710597)
XLA Ops:
  0.0 102.9 %mla_decode.1 = bf16[64,2,16,512]{3,2,1,0:T(8,128)(2,1)S(1)} custom-call(s32[64]{0:T(128)} %len_hbm.1, bf16[64,2,16,576]{3,2,1,0:T(8,128)(2,1)} %q_hbm.1, bf16[64,2048,576]{2,1,0:T(8,128)(2,1)} %bitcast.kv_hbm), custom_call_target="tpu_custom_call" | custom-call | tf_op jit(solution)/shard_map/mla_decode/pallas_call | solution.py:367
  102.9 1.3 %copy.5 = bf16[64,2,16,512]{3,2,1,0:T(8,128)(2,1)} copy(bf16[64,2,16,512]{3,2,1,0:T(8,128)(2,1)S(1)} %mla_decode.1) | data formatting | bytes 4194304

commit v5 on v4

--- a/solution.py
+++ b/solution.py
@@ -16,8 +16,8 @@
 LANES = 128
 PAIR = 2
 FIRST = 2
-AHEAD = 8
-LSE_STEPS = 4
+AHEAD = 12
+MSG = 4
 DEPTH = 3
 MESH_ID = pl.DeviceIdType.MESH
 F32 = jnp.float32
@@ -69,14 +69,13 @@
     def pair(i):
         return pl.ds(PAIR * i, PAIR)
 
-    q_msgs = steps // 2 + 1
+    heads_of = ((0, 1), (1, 1), (2, 2), (4, 2), (6, 2))
+    q_msgs = steps // MSG + 3
 
     def q_send(m, dest):
         slot = (2, 1, 3)[dest]
-        if isinstance(m, int) and m < 2:
-            at = pl.ds(PAIR * m, PAIR)
-        else:
-            at = pl.ds(2 * PAIR * (m - 1), 2 * PAIR)
+        first, count = heads_of[m] if isinstance(m, int) and m < 5 else (MSG * (m - 3), MSG)
+        at = pl.ds(PAIR * first, PAIR * count)
         return pltpu.make_async_remote_copy(
             src_ref=q_msg.at[1 if dest == 2 else 0, at], dst_ref=q_msg.at[slot, at],
             send_sem=qs_sem.at[dest, m], recv_sem=qr_sem.at[slot - 1, m],
@@ -89,24 +88,22 @@
             send_sem=part_ssem.at[slot], recv_sem=part_rsem.at[i],
             device_id={'dcp': partner}, device_id_type=MESH_ID)
 
-    out_msgs = steps // 2 + 1
+    groups = steps // MSG
+    long = groups - 2
+    last_of = ((steps - 8, 2), (steps - 6, 2), (steps - 4, 2), (steps - 2, 1), (steps - 1, 1))
 
     def out_send(m):
-        if isinstance(m, int) and m >= out_msgs - 2:
-            at = pl.ds(m + steps - out_msgs, 1)
-        else:
-            at = pl.ds(2 * m, 2)
+        first, count = last_of[m - long] if isinstance(m, int) and m >= long else (MSG * m, MSG)
+        at = pl.ds(first, count)
         return pltpu.make_async_remote_copy(
             src_ref=ici_send.at[at], dst_ref=ici_recv.at[at],
             send_sem=ici_ssem.at[0, m], recv_sem=ici_rsem.at[0, m],
             device_id={'dcp': across}, device_id_type=MESH_ID)
 
-    groups = steps // LSE_STEPS
-
     def lse_row(i):
         if isinstance(i, int) and i == steps - 1:
             return groups, 0
-        return i // LSE_STEPS, _mod(i, LSE_STEPS) // 2
+        return i // MSG, _mod(i, MSG) // 2
 
     def lse_send_copy(k):
         return pltpu.make_async_remote_copy(
@@ -134,7 +131,7 @@
         if k == 1:
             own_copies[1].wait()
             lax.fori_loop(1, cuts[2] // unroll, pack, 0)
-        for m in ((0, 1), range(2, AHEAD // 2 + 1))[k]:
+        for m in ((0, 1), range(2, AHEAD // MSG + 3))[k]:
             q_send(m, 1).start()
             q_send(m, 0).start()
     for i in range(DEPTH - 1):
@@ -148,6 +145,7 @@
     row_tok = lax.rem(lax.broadcasted_iota(jnp.int32, (group * rows, 1), 0) // heads, toks)
     col = lax.broadcasted_iota(jnp.int32, (1, seq_loc), 1)
     col_pos = (col // PAGE) * (group * PAGE) + lax.rem(col, PAGE) + me * PAGE
+    always = seq_loc // 2 - PAGE
     half = lax.broadcasted_iota(jnp.int32, (group * rows // 2, LANES), 1) < LANES // 2
 
     def load_q(b):
@@ -157,22 +155,24 @@
         rope = jnp.concatenate(
             [q_msg[g, b, toks * lat_tiles][:, t * ROPE:(t + 1) * ROPE]
              for g in range(group) for t in range(toks)], axis=0)
-        return lat, rope
+        return jnp.concatenate([lat, rope], axis=1)
 
     def scores(i, s, s_ref):
         slot = _mod(i, DEPTH)
         b = PAIR * i + s
-        lat, rope = load_q(b)
+        query = load_q(b)
         last = len_ref[b] - toks + row_tok
         best = None
         chunk = 512
         for n in range(seq_loc // chunk):
             at = pl.ds(n * chunk, chunk)
-            sc = _nt_dot(lat, kv_buf[slot, s, at, 0:LATENT]) + _nt_dot(rope, kv_buf[slot, s, at, LATENT:width])
-            sc = jnp.where(col_pos[:, n * chunk:(n + 1) * chunk] <= last, sc * scale2, MASKED)
-            s_ref[:, at] = sc
+            sc = _nt_dot(query, kv_buf[slot, s, at, :])
             for t in range(chunk // tile):
-                piece = sc[:, t * tile:(t + 1) * tile]
+                lo = n * chunk + t * tile
+                piece = sc[:, t * tile:(t + 1) * tile] * scale2
+                if lo + tile > always:
+                    piece = jnp.where(col_pos[:, lo:lo + tile] <= last, piece, MASKED)
+                s_ref[:, lo:lo + tile] = piece
                 best = piece if best is None else jnp.maximum(best, piece)
         return jnp.max(best, axis=1, keepdims=True)
 
@@ -220,9 +220,10 @@
         before = lse_send[k, pl.ds(r, 1)]
         lse_send[k, pl.ds(r, 1)] = jnp.where(lane_id[0:1] // (PAIR * rows) == _mod(i, 2), line, before)
 
-    def finish(i):
+    def finish_weights(i):
         k, r = lse_row(i)
         row = jnp.broadcast_to(lse_recv[k, pl.ds(r, 1)], (rows, LANES))
+        weights = []
         for s in range(PAIR):
             lane = row_id + (s * rows + PAIR * rows * _mod(i, 2))
             lse_b = jnp.sum(jnp.where(lane_id == lane, row, 0.0), axis=1, keepdims=True)
@@ -230,15 +231,21 @@
             m = jnp.maximum(lse_a, lse_b)
             w_a, w_b = jnp.exp2(lse_a - m), jnp.exp2(lse_b - m)
             inv = 1.0 / (w_a + w_b)
-            o = mine[i, s] * (w_a * inv) + ici_recv[i, s].astype(F32) * (w_b * inv)
+            weights.append((w_a * inv, w_b * inv))
+        return weights
+
+    def finish(i, weights=None):
+        weights = finish_weights(i) if weights is None else weights
+        for s in range(PAIR):
+            o = mine[i, s] * weights[s][0] + ici_recv[i, s].astype(F32) * weights[s][1]
             out_buf[PAIR * i + s] = o.astype(BF16).reshape(toks, heads, LATENT)
 
-    def when(i, parity, limit, action):
+    def when(i, phase, limit, action):
         if isinstance(i, int):
-            if i % 2 == parity and i < limit:
+            if i % MSG == phase and i < limit:
                 action()
         else:
-            pl.when(jnp.logical_and(lax.rem(i, 2) == parity, i < limit))(action)
+            pl.when(jnp.logical_and(lax.rem(i, MSG) == phase, i < limit))(action)
 
     def step(i, compute=True, merging=True):
         if merging:
@@ -254,18 +261,17 @@
                     kv_copy(i + DEPTH - 1, s).start()
 
             def more():
-                m = (i + AHEAD) // 2 + 1
+                m = (i + AHEAD) // MSG + 3
                 q_send(m, 1).start()
                 q_send(m, 0).start()
 
-            def forward():
-                m = (i + 1) // 2 + 1
+            def forward(m):
                 q_send(m, 1).wait_recv()
                 q_send(m, 2).start()
 
-            def arrived():
-                q_send(i // 2 + 1, 0).wait_recv()
-                q_send(i // 2 + 1, 2).wait_recv()
+            def arrived(m):
+                q_send(m, 0).wait_recv()
+                q_send(m, 2).wait_recv()
 
             if isinstance(i, int):
                 if i + DEPTH - 1 < steps:
@@ -273,16 +279,18 @@
             else:
                 pl.when(i + DEPTH - 1 < steps)(prefetch)
             when(i, 0, steps - AHEAD, more)
-            if isinstance(i, int) and i == 0:
-                q_send(1, 1).wait_recv()
-                q_send(1, 2).start()
+            if isinstance(i, int):
+                if i < 2:
+                    forward(i + 1)
+                arrived(i)
             else:
-                when(i, 1, steps - 1, forward)
-            if isinstance(i, int) and i < 2:
-                for dest in (0, 2):
-                    q_send(i, dest).wait_recv()
-            else:
-                when(i, 0, steps, arrived)
+                for m in (3, 4):
+                    pl.when(i == heads_of[m][0] - 1)(functools.partial(forward, m))
+                    pl.when(i == heads_of[m][0])(functools.partial(arrived, m))
+                late = i > heads_of[4][0]
+                pl.when(jnp.logical_and(late, jnp.logical_and(lax.rem(i, MSG) == MSG - 1, i < steps - 1)))(
+                    lambda: forward((i + 1) // MSG + 3))
+                pl.when(jnp.logical_and(late, lax.rem(i, MSG) == 0))(lambda: arrived(i // MSG + 3))
         if merging:
             merge(i - 2)
         if compute:
@@ -291,16 +299,9 @@
             attend(i, 1, s_b, p_b, tops[1])
 
     def send_out(i):
-        out_send(i // 2 - 2).start()
-
-        def send_lse():
-            lse_send_copy((i - 2) // LSE_STEPS - 1).start()
-
-        if isinstance(i, int):
-            if (i - 2) % LSE_STEPS == 0:
-                send_lse()
-        else:
-            pl.when(lax.rem(i - 2, LSE_STEPS) == 0)(send_lse)
+        k = (i - 2) // MSG - 1
+        out_send(k).start()
+        lse_send_copy(k).start()
 
     q_send(0, 1).wait_recv()
     q_send(0, 2).start()
@@ -309,49 +310,60 @@
     step(2)
 
     def body(i, carry):
-        when(i, 0, steps, lambda: send_out(i))
+        pl.when(jnp.logical_and(lax.rem(i, MSG) == 2, jnp.logical_and(i > MSG, i < steps - 4)))(lambda: send_out(i))
+        pl.when(i == steps - 4)(out_send(long).start)
+
+        @pl.when(i == steps - 2)
+        def _():
+            out_send(long + 1).start()
+            lse_send_copy(long).start()
+
         step(i)
         return carry
 
     lax.fori_loop(3, steps, body, 0)
-    send_out(steps)
+    out_send(long + 2).start()
     step(steps, compute=False)
     part_copy(steps - 1).wait()
     merge(steps - 1)
     lse_send_copy(groups - 1).start()
-    out_send(out_msgs - 2).start()
+    out_send(long + 3).start()
     lse_send_copy(groups).start()
-    out_send(out_msgs - 1).start()
-
-    for dest in range(3):
-        for m in range(2):
-            q_send(m, dest).wait_send()
+    out_send(long + 4).start()
 
     def q_sent(m, carry):
         for dest in range(3):
             q_send(m, dest).wait_send()
         return carry
 
-    lax.fori_loop(2, q_msgs, q_sent, 0)
+    for m in range(5):
+        q_sent(m, 0)
+    lax.fori_loop(5, q_msgs, q_sent, 0)
 
     def tail(k, carry):
-        for u in range(LSE_STEPS // 2):
-            out_send(LSE_STEPS // 2 * k + u).wait()
+        out_send(k).wait()
         lse_send_copy(k).wait()
-        for u in range(LSE_STEPS):
-            finish(LSE_STEPS * k + u)
+        for u in range(MSG):
+            finish(MSG * k + u)
         return carry
 
-    lax.fori_loop(0, groups - 1, tail, 0)
-    out_send(out_msgs - 3).wait()
+    lax.fori_loop(0, long, tail, 0)
+    out_send(long).wait()
+    out_send(long + 1).wait()
+    lse_send_copy(long).wait()
+    for i in range(steps - 8, steps - 4):
+        finish(i)
+    out_send(long + 2).wait()
     lse_send_copy(groups - 1).wait()
-    for i in range(steps - LSE_STEPS, steps - 2):
+    for i in range(steps - 4, steps - 2):
         finish(i)
-    out_send(out_msgs - 2).wait()
-    finish(steps - 2)
+    weights = finish_weights(steps - 2)
+    out_send(long + 3).wait()
+    finish(steps - 2, weights)
     lse_send_copy(groups).wait()
-    out_send(out_msgs - 1).wait()
-    finish(steps - 1)
+    weights = finish_weights(steps - 1)
+    out_send(long + 4).wait()
+    finish(steps - 1, weights)
 
 
 def solution(mesh):
@@ -389,16 +401,16 @@
                 pltpu.VMEM((steps, PAIR, rows, LANES), F32),
                 pltpu.VMEM((steps, PAIR, rows, LATENT), BF16),
                 pltpu.VMEM((steps, PAIR, rows, LATENT), BF16),
-                pltpu.VMEM((steps // LSE_STEPS + 1, LSE_STEPS // 2, LANES), F32),
-                pltpu.VMEM((steps // LSE_STEPS + 1, LSE_STEPS // 2, LANES), F32),
+                pltpu.VMEM((steps // MSG + 1, MSG // 2, LANES), F32),
+                pltpu.VMEM((steps // MSG + 1, MSG // 2, LANES), F32),
                 dma((4,)),
                 dma((DEPTH, PAIR)),
-                dma((3, steps // 2 + 1)),
-                dma((3, steps // 2 + 1)),
+                dma((3, steps // MSG + 3)),
+                dma((3, steps // MSG + 3)),
                 dma((2,)),
                 dma((steps,)),
-                dma((2, steps // 2 + 1)),
-                dma((2, steps // 2 + 1)),
+                dma((2, steps // MSG + 3)),
+                dma((2, steps // MSG + 3)),
             ],
             compiler_params=pltpu.CompilerParams(
                 collective_id=0, has_side_effects=True, vmem_limit_bytes=60_000_000),

time: 104 us -> 104 us (level)
  no operation moved by 1% of the time
where the time goes in v5:
time: 104 us
  Pallas kernels  102 us (98%)
  local copies, waits for them, and re-layouts  1.32 us (1%)
    pallas_call x1, Pallas kernels, local_step(): pl.pallas_call(_kernel, out_shape=pltpu.VMEM((batch, toks, heads, LATENT)...  102 us

profile of v5, /device:TPU:0, one launch (start us, length us, event | category | flops | bytes accessed | tf_op | source)
XLA Modules:
  0.0 103.6 jit_solution(18292511192205205277)
XLA Ops:
  0.0 102.3 %mla_decode.1 = bf16[64,2,16,512]{3,2,1,0:T(8,128)(2,1)S(1)} custom-call(s32[64]{0:T(128)} %len_hbm.1, bf16[64,2,16,576]{3,2,1,0:T(8,128)(2,1)} %q_hbm.1, bf16[64,2048,576]{2,1,0:T(8,128)(2,1)} %bitcast.kv_hbm), custom_call_target="tpu_custom_call" | custom-call | tf_op jit(solution)/shard_map/mla_decode/pallas_call | solution.py:379
  102.3 1.3 %copy.5 = bf16[64,2,16,512]{3,2,1,0:T(8,128)(2,1)} copy(bf16[64,2,16,512]{3,2,1,0:T(8,128)(2,1)S(1)} %mla_decode.1) | data formatting | bytes 4194304

commit v6 on v5

--- a/solution.py
+++ b/solution.py
@@ -12,7 +12,7 @@
 ROPE = 64
 NOPE = 128
 PAGE = 64
-MASKED = -1e30
+MASKED = -math.inf
 LANES = 128
 PAIR = 2
 FIRST = 2

time: 104 us -> 104 us (level)
  no operation moved by 1% of the time
where the time goes in v6:
time: 104 us
  Pallas kernels  102 us (98%)
  local copies, waits for them, and re-layouts  1.32 us (1%)
    pallas_call x1, Pallas kernels, local_step(): pl.pallas_call(_kernel, out_shape=pltpu.VMEM((batch, toks, heads, LATENT)...  102 us

profile of v6, /device:TPU:0, one launch (start us, length us, event | category | flops | bytes accessed | tf_op | source)
XLA Modules:
  0.0 103.6 jit_solution(12397550652706921579)
XLA Ops:
  0.0 102.3 %mla_decode.1 = bf16[64,2,16,512]{3,2,1,0:T(8,128)(2,1)S(1)} custom-call(s32[64]{0:T(128)} %len_hbm.1, bf16[64,2,16,576]{3,2,1,0:T(8,128)(2,1)} %q_hbm.1, bf16[64,2048,576]{2,1,0:T(8,128)(2,1)} %bitcast.kv_hbm), custom_call_target="tpu_custom_call" | custom-call | tf_op jit(solution)/shard_map/mla_decode/pallas_call | solution.py:379
  102.3 1.3 %copy.5 = bf16[64,2,16,512]{3,2,1,0:T(8,128)(2,1)} copy(bf16[64,2,16,512]{3,2,1,0:T(8,128)(2,1)S(1)} %mla_decode.1) | data formatting | bytes 4194304
